TPU v7x, 256 devices: a whole 4x4x8 slice. The times are simulated.
256 devices in a mesh: src: 32 (over y_lo, z, core), tgt: 8 (over x, y_hi).
Axes of the slice: x: 4, y: 4 (y_hi: 2, y_lo: 2; y = y_hi * 2 + y_lo), z: 8, core: 2. Of those that a mesh axis runs over, the one named last changes fastest.
Arguments:
- atom_feats: bfloat16 [2048, 3200], P(('src', 'tgt')), may hold values from -6 to 6
- positions: float32 [3, 2048], P(None, ('src', 'tgt')), may hold values from 0 to 1
- edge_src: int32 [262144], P(('src', 'tgt')), may hold values from 0 to 63
- edge_tgt: int32 [262144], P(('src', 'tgt')), may hold values from 0 to 255
- edge_angle: float32 [262144], P(('src', 'tgt')), may hold values from -3.140625 to 3.140625
- edge_scale: float32 [262144], P(('src', 'tgt')), may hold values from 0.1 to 1
- edge_count: int32 [32, 8], replicated, may hold values from 1 to 1024, as said below
- k_index: int32 [3, 2048], replicated, may hold values from -6 to 6
- k_filter: float32 [2048, 128], replicated, may hold values from -6 to 6
- weight_zero: bfloat16 [2, 640, 640], replicated, may hold values from -0.25 to 0.25
- weight_first: bfloat16 [2, 2, 512, 512], replicated, may hold values from -0.1875 to 0.1875
- weight_second: bfloat16 [2, 2, 384, 384], replicated, may hold values from -0.21875 to 0.21875
- weight_third: bfloat16 [2, 2, 256, 256], replicated, may hold values from -0.25 to 0.25
- weight_fourth: bfloat16 [2, 2, 128, 128], replicated, may hold values from -0.375 to 0.375
Outputs:
- edge_update: bfloat16 [2048, 3200], P(('tgt', 'src'))
- long_range: float32 [2048, 128], P(('src', 'tgt'))
Inputs may be any that keep to these rules, and one draw needn't show every extreme that they name: `edge_count`: live edge slots of tile (s, t); in every draw some tile is full with 1024.
All inputs are finite; a program needn't handle non-finite values.
Results may differ from a plain program's by a relative error of at most 0.0047.
Values may be sent and summed in bfloat16 or wider, within the bound.
No kernel may reach another device: no remote copies, remote signals or barrier semaphores. Data moves between devices by JAX's collectives and lax.ppermute only.
A program may use at most 64 MiB of HBM per device.

v0:
```python
import math
import jax
import jax.numpy as jnp
from jax import lax
from jax.sharding import PartitionSpec as P


def rotate(values, angles, handed, channels, degrees):
    pieces = [values[:, : (degrees + 1) * channels]]
    offset = (degrees + 1) * channels
    for degree in range(1, degrees + 1):
        columns = (degrees + 1 - degree) * channels
        cosine = jnp.cos(degree * angles)[:, None]
        sine_part = handed * jnp.sin(degree * angles)[:, None]
        leading = values[:, offset : offset + columns]
        trailing = values[:, offset + columns : offset + 2 * columns]
        pieces.append(cosine * leading + sine_part * trailing)
        pieces.append(cosine * trailing - sine_part * leading)
        offset += 2 * columns
    return jnp.concatenate(pieces, axis=1)


def pair_matrix(weights, conv_index):
    upper_half = jnp.concatenate([weights[conv_index, 0], weights[conv_index, 1]], axis=1)
    lower_half = jnp.concatenate([-weights[conv_index, 1], weights[conv_index, 0]], axis=1)
    return jnp.concatenate([upper_half, lower_half], axis=0)


def convolve(inputs, matrices):
    outputs = []
    offset = 0
    for matrix in matrices:
        height = matrix.shape[0]
        outputs.append(
            jnp.dot(inputs[:, offset : offset + height], matrix, preferred_element_type=jnp.float32)
        )
        offset += height
    return jnp.concatenate(outputs, axis=1)


def phase_table(coords, k_index):
    k_float = k_index.astype(jnp.float32)
    return (
        2.0
        * math.pi
        * (
            coords[0][:, None] * k_float[0][None, :]
            + coords[1][:, None] * k_float[1][None, :]
            + coords[2][:, None] * k_float[2][None, :]
        )
    )


def highest_dot(left_side, right_side):
    return jnp.dot(
        left_side, right_side, precision=lax.Precision.HIGHEST, preferred_element_type=jnp.float32
    )


def body(
    atom_feats,
    positions,
    edge_src,
    edge_tgt,
    edge_angle,
    edge_scale,
    edge_count,
    k_index,
    k_filter,
    weight_zero,
    weight_first,
    weight_second,
    weight_third,
    weight_fourth,
):
    channels = k_filter.shape[1]
    degrees = 4
    capacity = edge_src.shape[0]
    source_count = lax.axis_size("src")
    target_count = lax.axis_size("tgt")
    own_atoms = atom_feats.shape[0]
    target_rows = own_atoms * source_count
    feat_columns = atom_feats.shape[1]
    source_group = lax.axis_index("src")
    target_group = lax.axis_index("tgt")
    sections = []
    for conv_index in (0, 1):
        sections.append(
            [weight_zero[conv_index]]
            + [
                pair_matrix(weights, conv_index)
                for weights in (weight_first, weight_second, weight_third, weight_fourth)
            ]
        )
    block_feats = lax.all_gather(atom_feats, "tgt", axis=0, tiled=True)
    step_rows = math.gcd(256, capacity // 2)
    lane_ids = jnp.arange(step_rows, dtype=jnp.int32)
    target_ids = jnp.arange(target_rows, dtype=jnp.int32)

    def edge_message(edge_rows, angles, scales):
        turned = rotate(edge_rows.astype(jnp.float32), angles, 1.0, channels, degrees).astype(
            jnp.bfloat16
        )
        hidden = jax.nn.gelu(convolve(turned, sections[0]), approximate=False).astype(jnp.bfloat16)
        second = convolve(hidden, sections[1])
        return rotate(second, angles, -1.0, channels, degrees) * scales[:, None]

    def own_rows(first_slot):
        return jnp.take(
            block_feats, lax.dynamic_slice_in_dim(edge_src, first_slot, step_rows), axis=0
        )

    count_here = edge_count[source_group, target_group]
    zeros_total = jnp.zeros((target_rows, feat_columns), jnp.float32)

    def one_block(block_number, carried):
        first_slot = block_number * step_rows
        edge_rows = own_rows(first_slot)
        angles = lax.dynamic_slice_in_dim(edge_angle, first_slot, step_rows)
        scales = lax.dynamic_slice_in_dim(edge_scale, first_slot, step_rows)
        targets = lax.dynamic_slice_in_dim(edge_tgt, first_slot, step_rows)
        slot_ids = first_slot + lane_ids
        live_mask = ((slot_ids >= 0) & (slot_ids < count_here)).astype(jnp.float32)
        messages = edge_message(edge_rows, angles, scales) * live_mask[:, None]
        one_hot = (targets[:, None] == target_ids[None, :]).astype(jnp.float32)
        added = lax.dot_general(
            one_hot,
            messages,
            (((0,), (0,)), ((), ())),
            precision=lax.Precision.HIGHEST,
            preferred_element_type=jnp.float32,
        )
        return carried + added

    totals = lax.fori_loop(0, (count_here + step_rows - 1) // step_rows, one_block, zeros_total)
    edge_update = lax.psum_scatter(totals, "src", scatter_dimension=0, tiled=True).astype(
        jnp.bfloat16
    )
    total_atoms = own_atoms * source_count * target_count
    norm_factor = 1.0 / math.sqrt(total_atoms * k_filter.shape[0])
    phase = phase_table(positions, k_index)
    cos_table = jnp.cos(phase)
    sin_table = jnp.sin(phase)
    charges = atom_feats[:, :channels].astype(jnp.float32)
    factors_cos, factors_sin = lax.psum(
        (highest_dot(cos_table.T, charges), highest_dot(sin_table.T, charges)), ("src", "tgt")
    )
    summed = highest_dot(cos_table, k_filter * factors_cos) + highest_dot(
        sin_table, k_filter * factors_sin
    )
    long_range = summed * norm_factor
    return (edge_update, long_range)


def solution(mesh):
    return jax.shard_map(
        body,
        mesh=mesh,
        in_specs=(
            P(("src", "tgt"), None),
            P(None, ("src", "tgt")),
            P(("src", "tgt")),
            P(("src", "tgt")),
            P(("src", "tgt")),
            P(("src", "tgt")),
            P(),
            P(),
            P(),
            P(),
            P(),
            P(),
            P(),
            P(),
        ),
        out_specs=(P(("tgt", "src"), None), P(("src", "tgt"), None)),
        check_vma=False,
    )
```

profile of v0, /device:TPU:8, one launch (start us, length us, event | category | flops | bytes accessed | tf_op | source)
XLA Modules:
  0.0 330.4 jit_solution(7613350348428769478)
XLA Ops:
  7.2 0.8 slice_bitcast_fusion.20
  8.0 0.8 convert_element_type.28
  8.8 2.9 fusion.53
  11.8 2.9 fusion.50
  14.7 1.5 dynamic_slice.19
  16.9 0.7 slice_bitcast_fusion.14
  17.6 34.9 %all_gather.3 = bf16[64,3200]{1,0:T(8,128)(2,1)S(1)} all-gather(bf16[8,3200]{1,0:T(8,128)(2,1)S(1)} %copy-done.29), channel_id=1, replica_groups=mesh['src'=32,'tgt'=8] {'tgt'}, dimensions={0}, use_global_device_ids=true | all-gather | bytes 460800 | tf_op jit(solution)/shard_map/all_gather | solution.py:95
  52.4 0.7 fusion.92
  53.1 0.8 slice_bitcast_fusion.10
  53.9 1.9 fusion.94
  55.9 2.3 slice_bitcast_fusion.6
  58.2 0.9 fusion.96
  59.0 1.4 slice_bitcast_fusion.2
  60.5 2.8 slice_bitcast_fusion
  63.4 1.1 maximum_maximum_fusion.4
  64.5 2.8 maximum_maximum_fusion.2
  67.3 5.8 %maximum_maximum_fusion = (bf16[1024,1024]{1,0:T(8,128)(2,1)}, bf16[1024,1024]{1,0:T(8,128)(2,1)}) fusion(bf16[512,512]{1,0:T(8,128)(2,1)} %get-tuple-element.309, bf16[512,512]{1,0:T(8,128)(2,1)S(1)} %copy-done.10, bf16[512,512]{1,0:T(8,128)(2,1)} %get-tuple-element.308, bf16[512,512]{1,0:T(8,128)(2,1)} %get-tuple-element.310, ...), kind=kLoop, calls=%fused_computation.92 | loop fusion | flops 16777216 | bytes 7340032 | tf_op jit(solution)/shard_map/concatenate | solution.py:26
  73.1 1.9 broadcast.175
  75.0 29.6 %while.13 = (s32[]{:T(128)}, f32[256,3200]{1,0:T(8,128)}, s32[]{:T(128)}, s32[1024]{0:T(1024)}, s32[1024]{0:T(1024)}, /*index=5*/bf16[64,3200]{1,0:T(8,128)(2,1)...) while((s32[]{:T(128)}, f32[256,3200]{1,0:T(8,128)}, ...), condition=%wide.region_1.2_spmd.clone.clone, body=%wide.region_0.1_spmd.clone.clone.sunk | while | flops 5013903360 | bytes 114246840 | solution.py:135
  75.0 1.3 dynamic_slice.35
  76.3 1.3 dynamic_slice.36
  77.6 2.0 compare_and_fusion.2
  79.6 0.8 broadcast_multiply_fusion.7
  80.4 0.6 broadcast_multiply_fusion.8
  81.1 1.8 gather_fusion
  82.9 1.1 fusion.157
  84.5 0.2 add_convert_fusion.8
  84.7 0.4 copy-done.5
  85.1 0.5 convolution_dynamic-update-slice_fusion.12
  85.6 0.2 copy-done.11
  85.8 0.7 convolution_dynamic-update-slice_fusion.13
  86.6 0.5 convolution_dynamic-update-slice_fusion.14
  87.1 0.3 convolution_dynamic-update-slice_fusion.15
  87.6 7.2 %fusion.158 = bf16[256,3200]{1,0:T(8,128)(2,1)S(1)} fusion(f32[256,3200]{1,0:T(8,128)S(1)} %convolution_dynamic-update-slice_fusion.16), kind=kLoop, calls=%fused_computation.6.clone.1 | loop fusion | flops 53248000 | bytes 4915200 | tf_op jit(solution)/shard_map/while/body/convert_element_type | solution.py:104
  94.8 0.2 fusion.162
  95.0 0.3 fusion.161
  95.3 0.5 fusion.160
  95.8 0.6 copy-done.2
  96.4 0.7 fusion.159
  97.1 0.5 convolution_dynamic-update-slice_fusion.17
  98.7 0.9 copy-done
  99.6 3.3 convolution_add_fusion.3
  102.9 1.7 copy-done.1
  104.6 212.1 %all-reduce.6 = bf16[256,3200]{1,0:T(8,128)(2,1)S(1)} all-reduce(f32[256,3200]{1,0:T(8,128)} %get-tuple-element.155), channel_id=2, replica_groups=mesh['src'=32,'tgt'=8] {'src'}, use_global_device_ids=true, to_apply=%region_2.3.clone | all-reduce | flops 819200 | bytes 4915200
  316.7 0.6 dynamic-slice
  318.0 0.6 dynamic-slice_convert_fusion
  318.6 2.1 fusion.45
  320.8 2.8 fusion.43
  (89 shorter events, 2.0 us)
Async XLA Ops:
  7.2 10.4 %copy-start.29 = (bf16[8,3200]{1,0:T(8,128)(2,1)S(1)}, bf16[8,3200]{1,0:T(8,128)(2,1)}, u32[]{:S(2)}) copy-start(bf16[8,3200]{1,0:T(8,128)(2,1)} %param.16) | copy-start | bytes 153604
  7.2 9.7 %copy-start.19 = (bf16[2,2,128,128]{3,2,1,0:T(8,128)(2,1)S(1)}, bf16[2,2,128,128]{3,2,1,0:T(8,128)(2,1)}, u32[]{:S(2)}) copy-start(bf16[2,2,128,128]{3,2,1,0:T(8,128)(2,1)} %param.29) | copy-start | bytes 393220
  7.2 45.3 %copy-start.13 = (bf16[2,2,256,256]{3,2,1,0:T(8,128)(2,1)S(1)}, bf16[2,2,256,256]{3,2,1,0:T(8,128)(2,1)}, u32[]{:S(2)}) copy-start(bf16[2,2,256,256]{3,2,1,0:T(8,128)(2,1)} %param.28) | copy-start | bytes 1572868
  7.2 311.4 %all-reduce.5.cloned.1.call-start = ((), (), s32[]{:S(2)}) async-start(), calls=%async_computation | async-start | bytes 4194304 | tf_op jit(solution)/shard_map/psum | solution.py:145
  8.0 8.8 %copy-start.30 = (f32[8]{0:T(128)}, f32[8]{0:T(128)S(1)}, u32[]{:S(2)}) copy-start(f32[8]{0:T(128)S(1)} %get-tuple-element.336) | copy-start | bytes 100
  8.0 8.8 %copy-start.32 = (f32[8]{0:T(128)}, f32[8]{0:T(128)S(1)}, u32[]{:S(2)}) copy-start(f32[8]{0:T(128)S(1)} %get-tuple-element.337) | copy-start | bytes 100
  8.0 8.9 %copy-start.34 = (f32[8]{0:T(128)}, f32[8]{0:T(128)S(1)}, u32[]{:S(2)}) copy-start(f32[8]{0:T(128)S(1)} %get-tuple-element.338) | copy-start | bytes 100
  14.6 43.5 %copy-start.8 = (bf16[2,2,512,512]{3,2,1,0:T(8,128)(2,1)S(1)}, bf16[2,2,512,512]{3,2,1,0:T(8,128)(2,1)}, u32[]{:S(2)}) copy-start(bf16[2,2,512,512]{3,2,1,0:T(8,128)(2,1)} %param.26) | copy-start | bytes 6291460
  60.4 2.9 copy-start.20
  60.4 2.9 copy-start.21
  60.4 2.9 copy-start.22
  60.4 3.0 copy-start.14
  60.4 3.0 copy-start.15
  60.4 3.0 copy-start.16
  60.5 3.0 copy-start.17
  60.5 3.0 copy-start.18
  60.5 4.1 %copy-start.12 = (bf16[384,384]{1,0:T(8,128)(2,1)S(1)}, bf16[384,384]{1,0:T(8,128)(2,1)}, u32[]{:S(2)}) copy-start(bf16[384,384]{1,0:T(8,128)(2,1)} %get-tuple-element.315) | copy-start | bytes 884740
  63.3 4.0 %copy-start.10 = (bf16[512,512]{1,0:T(8,128)(2,1)S(1)}, bf16[512,512]{1,0:T(8,128)(2,1)}, u32[]{:S(2)}) copy-start(bf16[512,512]{1,0:T(8,128)(2,1)} %get-tuple-element.312) | copy-start | bytes 1572868
  82.9 1.1 copy-start.28
  82.9 1.3 copy-start.27
  82.9 1.4 copy-start.26
  84.0 1.1 copy-start.5
  84.0 1.8 copy-start.11
  85.8 1.2 copy-start.6
  87.4 7.6 %copy-start.7 = (bf16[512,512]{1,0:T(8,128)(2,1)S(1)}, bf16[512,512]{1,0:T(8,128)(2,1)}, u32[]{:S(2)}) copy-start(bf16[512,512]{1,0:T(8,128)(2,1)} %get-tuple-element.574) | copy-start | bytes 1572868 | tf_op jit(solution)/shard_map/while
  87.6 7.7 %copy-start.3 = (bf16[768,768]{1,0:T(8,128)(2,1)S(1)}, bf16[768,768]{1,0:T(8,128)(2,1)}, u32[]{:S(2)}) copy-start(bf16[768,768]{1,0:T(8,128)(2,1)} %get-tuple-element.573) | copy-start | bytes 3538948 | tf_op jit(solution)/shard_map/while
  94.8 1.6 copy-start.2
  95.3 1.8 copy-start.4
  97.7 1.9 copy-start
  97.7 1.9 copy-start.23
  97.7 1.9 copy-start.24
  97.7 1.9 copy-start.25
  102.9 1.7 copy-start.1
  104.6 212.2 %copy-start.36 = (u32[256]{0:T(256)S(1)}, u32[256]{0:T(256)}, u32[]{:S(2)}) copy-start(u32[256]{0:T(256)} %constant.174) | copy-start | bytes 3076
  104.6 214.0 %copy-start.9 = (f32[2048,128]{1,0:T(8,128)S(1)}, f32[2048,128]{1,0:T(8,128)}, u32[]{:S(2)}) copy-start(f32[2048,128]{1,0:T(8,128)} %param.24) | copy-start | bytes 3145732
  104.6 214.0 %copy-start.31 = (f32[8]{0:T(128)S(1)}, f32[8]{0:T(128)}, u32[]{:S(2)}) copy-start(f32[8]{0:T(128)} %copy-done.30) | copy-start | bytes 100
  104.6 214.0 %copy-start.33 = (f32[8]{0:T(128)S(1)}, f32[8]{0:T(128)}, u32[]{:S(2)}) copy-start(f32[8]{0:T(128)} %copy-done.32) | copy-start | bytes 100
  104.6 214.0 %copy-start.35 = (f32[8]{0:T(128)S(1)}, f32[8]{0:T(128)}, u32[]{:S(2)}) copy-start(f32[8]{0:T(128)} %copy-done.34) | copy-start | bytes 100
Sparse Core Ops, SparseCore 0:
  14.8 267.9 all-reduce.4
where the time goes:
time: 332 us; the launch traced here: 330 us
  blocking collectives  247 us (74%)
  other arithmetic  27.4 us (8%)
  local copies, waits for them, and re-layouts  21.8 us (7%)
  matrix products  18.2 us (5%)
  between operations  15.6 us (5%)
    unnamed x1, blocking collectives  212 us
    all_gather x1, blocking collectives, body(): block_feats = lax.all_gather(atom_feats, 'tgt', axis=0, tiled=True)  34.9 us
    dot_general x4, matrix products, highest_dot(): jnp.dot(left_side, right_side, precision=lax.Precision.HIGHEST, preferred...  10.7 us
    concatenate x4, other arithmetic, pair_matrix(): return jnp.concatenate([upper_half, lower_half], axis=0)  9.71 us
    convert_element_type x1, other arithmetic, edge_message(): jax.nn.gelu(convolve(turned, sections[0]), approximate=False)  7.17 us
  transfers between devices with their start and end apart: 1, of which 0 were waited for; matrix products, arithmetic and copies ran while one was open for 15% of the time, Pallas kernels for 0%

commit v1 on v0

--- a/solution.py
+++ b/solution.py
@@ -92,7 +92,8 @@
                 for weights in (weight_first, weight_second, weight_third, weight_fourth)
             ]
         )
-    block_feats = lax.all_gather(atom_feats, "tgt", axis=0, tiled=True)
+    sent = jnp.stack([atom_feats] * lax.axis_size("tgt"))
+    block_feats = jnp.concatenate(lax.all_to_all(sent, "tgt", 0, 0), axis=0)
     step_rows = math.gcd(256, capacity // 2)
     lane_ids = jnp.arange(step_rows, dtype=jnp.int32)
     target_ids = jnp.arange(target_rows, dtype=jnp.int32)

time: 332 us -> 306 us (0.922)
  blocking collectives: 247 us -> 213 us
  starting transfers between devices: 0.04 us -> 6.07 us
    all_gather x1 -> x0, blocking collectives: 34.9 us -> none  [body(): block_feats = lax.all_gather(atom_feats, 'tgt', axis=0, tiled=True)]
    all_to_all x0 -> x1, starting transfers between devices: none -> 6.03 us  [body(): block_feats = jnp.concatenate(lax.all_to_all(sent, 'tgt', 0, 0), axis=0)]
  transfers between devices with their start and end apart: 1 -> 2, of which waited for: 0 -> 0; matrix products, arithmetic and copies ran while one was open for 15% -> 19% of each run, Pallas kernels for 0% -> 0%
where the time goes in v1:
time: 306 us; the launch traced here: 304 us
  blocking collectives  213 us (70%)
  other arithmetic  27.3 us (9%)
  local copies, waits for them, and re-layouts  23.5 us (8%)
  matrix products  18.2 us (6%)
  between operations  15.6 us (5%)
  starting transfers between devices  6.07 us (2%)
    unnamed x1, blocking collectives  213 us
    dot_general x4, matrix products, highest_dot(): jnp.dot(left_side, right_side, precision=lax.Precision.HIGHEST, preferred...  10.7 us
    concatenate x4, other arithmetic, pair_matrix(): return jnp.concatenate([upper_half, lower_half], axis=0)  9.71 us
    convert_element_type x1, other arithmetic, edge_message(): jax.nn.gelu(convolve(turned, sections[0]), approximate=False)  7.17 us
  transfers between devices with their start and end apart: 2, of which 0 were waited for; matrix products, arithmetic and copies ran while one was open for 19% of the time, Pallas kernels for 0%

profile of v1, /device:TPU:8, one launch (start us, length us, event | category | flops | bytes accessed | tf_op | source)
XLA Modules:
  0.0 304.2 jit_solution(17055466755658930581)
XLA Ops:
  7.2 1.6 stack.2
  8.8 6.0 %all-to-all-start = ((bf16[8,8,3200]{2,1,0:T(8,128)(2,1)}), bf16[8,8,3200]{2,1,0:T(8,128)(2,1)S(1)}, u32[]{:S(2)}, u32[]{:S(2)}) async-start(bf16[8,8,3200]{2,1,0:T(8,128)(2,1)} %stack.2), calls=%async_computation | async-start | bytes 819200 | tf_op jit(solution)/shard_map/all_to_all | solution.py:96
  14.9 0.8 slice_bitcast_fusion.20
  15.7 0.8 convert_element_type.28
  16.5 2.9 fusion.53
  19.4 2.9 fusion.50
  22.4 1.5 dynamic_slice.19
  24.5 0.6 slice_bitcast_fusion.14
  25.2 0.7 fusion.92
  25.9 0.8 slice_bitcast_fusion.10
  26.7 1.9 fusion.94
  28.6 2.3 slice_bitcast_fusion.6
  30.9 0.9 fusion.96
  31.8 1.4 slice_bitcast_fusion.2
  33.3 2.8 slice_bitcast_fusion
  36.1 0.6 dynamic-slice
  37.5 1.1 maximum_maximum_fusion.4
  38.6 2.8 maximum_maximum_fusion.2
  41.4 5.8 %maximum_maximum_fusion = (bf16[1024,1024]{1,0:T(8,128)(2,1)}, bf16[1024,1024]{1,0:T(8,128)(2,1)}) fusion(bf16[512,512]{1,0:T(8,128)(2,1)} %get-tuple-element.309, bf16[512,512]{1,0:T(8,128)(2,1)S(1)} %copy-done.10, bf16[512,512]{1,0:T(8,128)(2,1)} %get-tuple-element.308, bf16[512,512]{1,0:T(8,128)(2,1)} %get-tuple-element.310, ...), kind=kLoop, calls=%fused_computation.92 | loop fusion | flops 16777216 | bytes 7340032 | tf_op jit(solution)/shard_map/concatenate | solution.py:26
  47.2 1.9 broadcast.177
  49.0 29.6 %while.13 = (s32[]{:T(128)}, f32[256,3200]{1,0:T(8,128)}, s32[]{:T(128)}, s32[1024]{0:T(1024)}, s32[1024]{0:T(1024)}, /*index=5*/bf16[64,3200]{1,0:T(8,128)(2,1)...) while((s32[]{:T(128)}, f32[256,3200]{1,0:T(8,128)}, ...), condition=%wide.region_1.2_spmd.clone.clone, body=%wide.region_0.1_spmd.clone.clone.sunk | while | flops 5013903360 | bytes 114246840 | solution.py:136
  49.0 1.3 dynamic_slice.35
  50.4 1.3 dynamic_slice.36
  51.7 2.0 compare_and_fusion.2
  53.7 0.8 broadcast_multiply_fusion.7
  54.5 0.6 broadcast_multiply_fusion.8
  55.2 1.8 gather_fusion
  57.0 1.1 fusion.157
  58.6 0.2 add_convert_fusion.8
  58.8 0.4 copy-done.5
  59.2 0.5 convolution_dynamic-update-slice_fusion.12
  59.7 0.3 copy-done.11
  59.9 0.7 convolution_dynamic-update-slice_fusion.13
  60.7 0.5 convolution_dynamic-update-slice_fusion.14
  61.2 0.3 convolution_dynamic-update-slice_fusion.15
  61.7 7.2 %fusion.158 = bf16[256,3200]{1,0:T(8,128)(2,1)S(1)} fusion(f32[256,3200]{1,0:T(8,128)S(1)} %convolution_dynamic-update-slice_fusion.16), kind=kLoop, calls=%fused_computation.6.clone.1 | loop fusion | flops 53248000 | bytes 4915200 | tf_op jit(solution)/shard_map/while/body/convert_element_type | solution.py:105
  69.1 0.3 fusion.161
  69.4 0.5 fusion.160
  69.9 0.6 copy-done.2
  70.5 0.7 fusion.159
  71.2 0.5 convolution_dynamic-update-slice_fusion.17
  72.8 0.9 copy-done
  73.7 3.3 %convolution_add_fusion.3 = f32[256,3200]{1,0:T(8,128)S(1)} fusion(f32[256,3200]{1,0:T(8,128)S(1)} %copy-done, f32[256,3200]{1,0:T(8,128)S(1)} %subtract_dynamic-update-slice_fusion.11, f32[256]{0:T(256)S(1)} %copy-done.23, f32[256]{0:T(256)S(1)} %copy-done.24, s32[256]{0:T(256)S(1)} %copy-done.25), kind=kOutput, calls=%fused_computation.2.clone.1 | convolution fusion | flops 2519105536 | bytes 9833472 | tf_op jit(solution)/shard_map/while/body/dot_general | solution.py:127
  77.0 1.6 copy-done.1
  78.7 213.1 %all-reduce.6 = bf16[256,3200]{1,0:T(8,128)(2,1)S(1)} all-reduce(f32[256,3200]{1,0:T(8,128)} %get-tuple-element.155), channel_id=2, replica_groups=mesh['src'=32,'tgt'=8] {'src'}, use_global_device_ids=true, to_apply=%region_2.3.clone | all-reduce | flops 819200 | bytes 4915200
  291.8 0.6 dynamic-slice_convert_fusion
  292.4 2.1 fusion.45
  294.6 2.8 fusion.43
  (89 shorter events, 2.1 us)
Async XLA Ops:
  7.2 17.4 %copy-start.19 = (bf16[2,2,128,128]{3,2,1,0:T(8,128)(2,1)S(1)}, bf16[2,2,128,128]{3,2,1,0:T(8,128)(2,1)}, u32[]{:S(2)}) copy-start(bf16[2,2,128,128]{3,2,1,0:T(8,128)(2,1)} %param.29) | copy-start | bytes 393220
  7.2 18.0 %copy-start.13 = (bf16[2,2,256,256]{3,2,1,0:T(8,128)(2,1)S(1)}, bf16[2,2,256,256]{3,2,1,0:T(8,128)(2,1)}, u32[]{:S(2)}) copy-start(bf16[2,2,256,256]{3,2,1,0:T(8,128)(2,1)} %param.28) | copy-start | bytes 1572868
  8.8 38.3 %all-to-all-start = ((bf16[8,8,3200]{2,1,0:T(8,128)(2,1)}), bf16[8,8,3200]{2,1,0:T(8,128)(2,1)S(1)}, u32[]{:S(2)}, u32[]{:S(2)}) async-start(bf16[8,8,3200]{2,1,0:T(8,128)(2,1)} %stack.2), calls=%async_computation | async-start | bytes 819200 | tf_op jit(solution)/shard_map/all_to_all | solution.py:96
  14.9 277.5 %all-reduce.5.cloned.1.call-start = ((), (), s32[]{:S(2)}) async-start(), calls=%async_computation.1 | async-start | bytes 4194304 | tf_op jit(solution)/shard_map/psum | solution.py:146
  15.7 8.8 %copy-start.29 = (f32[8]{0:T(128)}, f32[8]{0:T(128)S(1)}, u32[]{:S(2)}) copy-start(f32[8]{0:T(128)S(1)} %get-tuple-element.336) | copy-start | bytes 100
  15.7 8.8 %copy-start.31 = (f32[8]{0:T(128)}, f32[8]{0:T(128)S(1)}, u32[]{:S(2)}) copy-start(f32[8]{0:T(128)S(1)} %get-tuple-element.337) | copy-start | bytes 100
  15.7 8.8 %copy-start.33 = (f32[8]{0:T(128)}, f32[8]{0:T(128)S(1)}, u32[]{:S(2)}) copy-start(f32[8]{0:T(128)S(1)} %get-tuple-element.338) | copy-start | bytes 100
  22.3 8.6 %copy-start.8 = (bf16[2,2,512,512]{3,2,1,0:T(8,128)(2,1)S(1)}, bf16[2,2,512,512]{3,2,1,0:T(8,128)(2,1)}, u32[]{:S(2)}) copy-start(bf16[2,2,512,512]{3,2,1,0:T(8,128)(2,1)} %param.26) | copy-start | bytes 6291460
  31.8 4.3 %copy-start.35 = (u32[256]{0:T(256)S(1)}, u32[256]{0:T(256)}, u32[]{:S(2)}) copy-start(u32[256]{0:T(256)} %constant.174) | copy-start | bytes 3076
  33.2 4.2 %copy-start.20 = (bf16[128,128]{1,0:T(8,128)(2,1)S(1)}, bf16[128,128]{1,0:T(8,128)(2,1)}, u32[]{:S(2)}) copy-start(bf16[128,128]{1,0:T(8,128)(2,1)} %get-tuple-element.328) | copy-start | bytes 98308
  33.2 4.2 %copy-start.21 = (bf16[128,128]{1,0:T(8,128)(2,1)S(1)}, bf16[128,128]{1,0:T(8,128)(2,1)}, u32[]{:S(2)}) copy-start(bf16[128,128]{1,0:T(8,128)(2,1)} %get-tuple-element.329) | copy-start | bytes 98308
  33.2 4.2 %copy-start.22 = (bf16[128,128]{1,0:T(8,128)(2,1)S(1)}, bf16[128,128]{1,0:T(8,128)(2,1)}, u32[]{:S(2)}) copy-start(bf16[128,128]{1,0:T(8,128)(2,1)} %get-tuple-element.330) | copy-start | bytes 98308
  33.2 4.2 %copy-start.14 = (bf16[256,256]{1,0:T(8,128)(2,1)S(1)}, bf16[256,256]{1,0:T(8,128)(2,1)}, u32[]{:S(2)}) copy-start(bf16[256,256]{1,0:T(8,128)(2,1)} %get-tuple-element.326) | copy-start | bytes 393220
  33.2 4.2 %copy-start.15 = (bf16[256,256]{1,0:T(8,128)(2,1)S(1)}, bf16[256,256]{1,0:T(8,128)(2,1)}, u32[]{:S(2)}) copy-start(bf16[256,256]{1,0:T(8,128)(2,1)} %get-tuple-element.321) | copy-start | bytes 393220
  33.2 4.2 %copy-start.16 = (bf16[256,256]{1,0:T(8,128)(2,1)S(1)}, bf16[256,256]{1,0:T(8,128)(2,1)}, u32[]{:S(2)}) copy-start(bf16[256,256]{1,0:T(8,128)(2,1)} %get-tuple-element.322) | copy-start | bytes 393220
  33.2 4.2 %copy-start.17 = (bf16[256,256]{1,0:T(8,128)(2,1)S(1)}, bf16[256,256]{1,0:T(8,128)(2,1)}, u32[]{:S(2)}) copy-start(bf16[256,256]{1,0:T(8,128)(2,1)} %get-tuple-element.323) | copy-start | bytes 393220
  33.2 4.2 %copy-start.18 = (bf16[256,256]{1,0:T(8,128)(2,1)S(1)}, bf16[256,256]{1,0:T(8,128)(2,1)}, u32[]{:S(2)}) copy-start(bf16[256,256]{1,0:T(8,128)(2,1)} %get-tuple-element.324) | copy-start | bytes 393220
  33.2 5.3 %copy-start.12 = (bf16[384,384]{1,0:T(8,128)(2,1)S(1)}, bf16[384,384]{1,0:T(8,128)(2,1)}, u32[]{:S(2)}) copy-start(bf16[384,384]{1,0:T(8,128)(2,1)} %get-tuple-element.315) | copy-start | bytes 884740
  36.1 5.3 %copy-start.10 = (bf16[512,512]{1,0:T(8,128)(2,1)S(1)}, bf16[512,512]{1,0:T(8,128)(2,1)}, u32[]{:S(2)}) copy-start(bf16[512,512]{1,0:T(8,128)(2,1)} %get-tuple-element.312) | copy-start | bytes 1572868
  57.0 1.1 copy-start.28
  57.0 1.3 copy-start.27
  57.0 1.4 copy-start.26
  58.1 1.1 copy-start.5
  58.1 1.9 copy-start.11
  59.9 1.2 copy-start.6
  61.5 7.6 %copy-start.7 = (bf16[512,512]{1,0:T(8,128)(2,1)S(1)}, bf16[512,512]{1,0:T(8,128)(2,1)}, u32[]{:S(2)}) copy-start(bf16[512,512]{1,0:T(8,128)(2,1)} %get-tuple-element.574) | copy-start | bytes 1572868 | tf_op jit(solution)/shard_map/while
  61.7 7.7 %copy-start.3 = (bf16[768,768]{1,0:T(8,128)(2,1)S(1)}, bf16[768,768]{1,0:T(8,128)(2,1)}, u32[]{:S(2)}) copy-start(bf16[768,768]{1,0:T(8,128)(2,1)} %get-tuple-element.573) | copy-start | bytes 3538948 | tf_op jit(solution)/shard_map/while
  68.9 1.6 copy-start.2
  69.4 1.8 copy-start.4
  71.8 1.9 copy-start
  71.8 1.9 copy-start.23
  71.8 1.9 copy-start.24
  71.8 1.9 copy-start.25
  77.0 1.7 copy-start.1
  78.7 213.7 %copy-start.9 = (f32[2048,128]{1,0:T(8,128)S(1)}, f32[2048,128]{1,0:T(8,128)}, u32[]{:S(2)}) copy-start(f32[2048,128]{1,0:T(8,128)} %param.24) | copy-start | bytes 3145732
  78.7 213.7 %copy-start.30 = (f32[8]{0:T(128)S(1)}, f32[8]{0:T(128)}, u32[]{:S(2)}) copy-start(f32[8]{0:T(128)} %copy-done.29) | copy-start | bytes 100
  78.7 213.7 %copy-start.32 = (f32[8]{0:T(128)S(1)}, f32[8]{0:T(128)}, u32[]{:S(2)}) copy-start(f32[8]{0:T(128)} %copy-done.31) | copy-start | bytes 100
  78.7 213.7 %copy-start.34 = (f32[8]{0:T(128)S(1)}, f32[8]{0:T(128)}, u32[]{:S(2)}) copy-start(f32[8]{0:T(128)} %copy-done.33) | copy-start | bytes 100
Sparse Core Ops, SparseCore 0:
  22.4 268.8 all-reduce.4
